TPU v7x, 32 devices: a whole 2x2x4 slice. The times are simulated.
32 devices in a mesh: rows: 8 (over z, y), sub: 4 (over x, core).
Axes of the slice: x: 2, y: 2, z: 4, core: 2. Of those that a mesh axis runs over, the one named last changes fastest.
Arguments:
- frames: float32 [15, 32768], P(None, ('rows', 'sub')), may hold values from -1 to 1, as said below
- start_vector: float32 [3, 32768], P(None, ('rows', 'sub')), may hold values from -12 to 12
- edge_blocks: float32 [36, 65536], P(None, ('rows', 'sub')), may hold values from -14.4 to 14.4
- edge_source: int32 [32, 2048], P(('rows', 'sub')), may hold values from 0 to 1023
- edge_target: int32 [32, 2048], P(('rows', 'sub')), may hold values from 0 to 1535, as said below
- edge_count: int32 [32], P(('rows', 'sub')), may hold values from 1024 to 2048, as said below
- send_index: int32 [32, 512], P(('rows', 'sub')), may hold values from 0 to 1024, as said below
Outputs:
- new_frames: float32 [15, 32768], P(None, ('rows', 'sub'))
- last_vector: float32 [3, 32768], P(None, ('rows', 'sub'))
- tridiagonal: float32 [2, 4], replicated
Inputs may be any that keep to these rules, and one draw needn't show every extreme that they name: `frames`: each pose's block has orthonormal columns to float32 rounding. `edge_target`: below 1024: a pose of the same device. 1024 + u: halo slot u, whose block u // 16 on the providing device is never empty. `edge_count`: some device uses all 2048 slots. `send_index`: row q holds, in blocks of 16, the local poses that device q provides to device p (block p); a block is all poses or all 1024, which marks it empty; a device's block for itself is empty.
All inputs are finite; a program needn't handle non-finite values.
Results may differ from a plain program's by a relative error of at most 0.0003.
Values sent between devices are 32-bit elements; how exact they have to be, the bound alone decides.
A program may use at most 64 MiB of HBM per device.

v0:
```python
import jax
import jax.numpy as jnp
from jax import lax
from jax.sharding import PartitionSpec as P

RANK = 5
DIM = 3
LANCZOS = 4
polar_steps = 8
step_length = 0.3
epsilon = 1e-06


def symmetric(edge_blocks):
    blocks_six = edge_blocks.reshape(6, 6, -1)
    return 0.5 * (blocks_six + blocks_six.transpose(1, 0, 2))


def block_product(matrix, field_in):
    return jnp.sum(matrix[None, :, :, :] * field_in[:, None, :, :], axis=2)


def multiplier(left_field, right_field):
    product = jnp.sum(left_field[:, :, None, :] * right_field[:, None, :, :], axis=0)
    return 0.5 * (product + product.transpose(1, 0, 2))


def right_product(field_in, matrix):
    return jnp.sum(field_in[:, :, None, :] * matrix[None, :, :, :], axis=1)


def take_columns(table, index):
    return jnp.take(table, index, axis=1, mode="fill", fill_value=0.0)


def add_columns(values, index, width):
    total = jnp.zeros((values.shape[0], width), jnp.float32)
    return total.at[:, index].add(values, mode="drop")


def pack_rows(field_in, send_row):
    flattened = field_in.reshape(-1, field_in.shape[-1])
    return take_columns(flattened, send_row)


def return_rows(returned, send_row, poses_here):
    return add_columns(returned, send_row, poses_here)


def edge_terms(field_in, halo_vals, coupling, source, target, weight):
    copies = field_in.shape[0]
    poses_here = field_in.shape[2]
    edge_total = source.shape[0]
    extended = jnp.concatenate([field_in, halo_vals.reshape(copies, DIM, -1)], axis=2)
    full_width = extended.shape[2]
    values_first = take_columns(field_in.reshape(copies * DIM, poses_here), source).reshape(
        copies, DIM, edge_total
    )
    values_second = take_columns(extended.reshape(copies * DIM, full_width), target).reshape(
        copies, DIM, edge_total
    )
    upper_part = block_product(coupling[:3, :3], values_first) + block_product(
        coupling[:3, 3:], values_second
    )
    lower_part = block_product(coupling[3:, :3], values_first) + block_product(
        coupling[3:, 3:], values_second
    )
    upper_sum = add_columns(
        (upper_part * weight).reshape(copies * DIM, edge_total), source, poses_here
    )
    lower_sum = add_columns(
        (lower_part * weight).reshape(copies * DIM, edge_total), target, full_width
    )
    home_part = (upper_sum + lower_sum[:, :poses_here]).reshape(copies, DIM, poses_here)
    far_part = lower_sum[:, poses_here:].reshape(copies, DIM, full_width - poses_here)
    return (home_part, far_part)


def retract(frame_now, gradient, length):
    moved = frame_now - length * gradient
    norms = jnp.sum(moved * moved, axis=(0, 1))
    polar_now = moved * jnp.sqrt(DIM / norms)[None, None, :]
    identity = jnp.eye(DIM, dtype=jnp.float32)[:, :, None]
    for iteration in range(polar_steps):
        gram_matrix = jnp.sum(polar_now[:, :, None, :] * polar_now[:, None, :, :], axis=0)
        polar_now = right_product(polar_now, 1.5 * identity - 0.5 * gram_matrix)
    return polar_now


def on_device(frames, start_vector, edge_blocks, edge_source, edge_target, edge_count, send_index):
    poses_here = frames.shape[1]
    shards = lax.axis_size("rows") * lax.axis_size("sub")
    coupling = symmetric(edge_blocks)
    source = edge_source[0]
    target = edge_target[0]
    send_row = send_index[0]
    weight = (jnp.arange(source.shape[0], dtype=jnp.int32) < edge_count[0]).astype(jnp.float32)

    def split_product(field_in, halo_vals):
        return edge_terms(field_in, halo_vals, coupling, source, target, weight)

    frame_now = frames.reshape(RANK, DIM, poses_here)
    halo_vals = lax.all_to_all(
        pack_rows(frame_now, send_row), ("rows", "sub"), split_axis=1, concat_axis=1, tiled=True
    )
    near_part, far_part = split_product(frame_now, halo_vals)
    returned = lax.all_to_all(
        far_part.reshape(RANK * DIM, -1), ("rows", "sub"), split_axis=1, concat_axis=1, tiled=True
    )
    euclidean = near_part + return_rows(returned, send_row, poses_here).reshape(
        RANK, DIM, poses_here
    )
    multipliers = multiplier(frame_now, euclidean)
    gradient = 2.0 * (euclidean - right_product(frame_now, multipliers))
    total_square = lax.psum(jnp.sum(gradient * gradient), ("rows", "sub"))
    length = (
        step_length * jnp.sqrt(jnp.float32(poses_here * shards)) / jnp.sqrt(total_square + epsilon)
    )
    retracted = retract(frame_now, gradient, length)
    halo_moved = lax.all_to_all(
        pack_rows(retracted, send_row), ("rows", "sub"), split_axis=1, concat_axis=1, tiled=True
    )
    near_moved, far_moved = split_product(retracted, halo_moved)
    returned_moved = lax.all_to_all(
        far_moved.reshape(RANK * DIM, -1), ("rows", "sub"), split_axis=1, concat_axis=1, tiled=True
    )
    product_new = near_moved + return_rows(returned_moved, send_row, poses_here).reshape(
        RANK, DIM, poses_here
    )
    certificate_mult = multiplier(retracted, product_new)
    entries = DIM * poses_here * shards
    start_square = lax.psum(jnp.sum(start_vector * start_vector), ("rows", "sub"))
    start_field = start_vector.reshape(1, DIM, poses_here)
    krylov_basis = [start_field / jnp.sqrt(start_square / entries + epsilon)]
    alpha_list = []
    beta_list = []
    for iteration in range(LANCZOS):
        vector = krylov_basis[-1]
        halo_vector = lax.all_to_all(
            pack_rows(vector, send_row), ("rows", "sub"), split_axis=1, concat_axis=1, tiled=True
        )
        near_vector, far_vector = split_product(vector, halo_vector)
        returned_vector = lax.all_to_all(
            far_vector.reshape(DIM, -1), ("rows", "sub"), split_axis=1, concat_axis=1, tiled=True
        )
        image_vec = near_vector + return_rows(returned_vector, send_row, poses_here).reshape(
            1, DIM, poses_here
        )
        image_vec = image_vec - right_product(vector, certificate_mult)
        local_dots = jnp.stack([jnp.sum(member * image_vec) for member in krylov_basis])
        summed_dots, square_total = lax.psum(
            (local_dots, jnp.sum(image_vec * image_vec)), ("rows", "sub")
        )
        projected = summed_dots / entries
        for position in range(len(krylov_basis)):
            image_vec = image_vec - projected[position] * krylov_basis[position]
        beta_now = jnp.sqrt(square_total / entries - jnp.sum(projected * projected) + epsilon)
        krylov_basis.append(image_vec / beta_now)
        alpha_list.append(projected[-1])
        beta_list.append(beta_now)
    tridiagonal = jnp.stack([jnp.stack(alpha_list), jnp.stack(beta_list)])
    return (
        retracted.reshape(RANK * DIM, poses_here),
        krylov_basis[-1].reshape(DIM, poses_here),
        tridiagonal,
    )


def solution(mesh):
    in_specs = (
        P(None, ("rows", "sub")),
        P(None, ("rows", "sub")),
        P(None, ("rows", "sub")),
        P(("rows", "sub"), None),
        P(("rows", "sub"), None),
        P(("rows", "sub")),
        P(("rows", "sub"), None),
    )
    out_specs = (P(None, ("rows", "sub")), P(None, ("rows", "sub")), P())
    return jax.shard_map(
        on_device, mesh=mesh, in_specs=in_specs, out_specs=out_specs, check_vma=False
    )
```

profile of v0, /device:TPU:0, one launch (start us, length us, event | category | flops | bytes accessed | tf_op | source)
XLA Modules:
  0.0 608.0 jit_solution(1578713201348669233)
XLA Ops:
  4.7 7.3 %all-to-all-start = ((f32[32,1,240]{2,1,0:T(1,128)}), f32[32,1,240]{2,1,0:T(1,128)S(1)}, u32[]{:S(2)}, u32[]{:S(2)}) async-start(f32[32,1,240]{2,1,0:T(1,128)} %reshape.1031), calls=%async_computation | async-start | bytes 65536 | tf_op jit(solution)/shard_map/all_to_all | solution.py:103
  31.8 11.7 %scatter_custom_fusion = f32[15,1536]{0,1:T(8,128)S(1)} fusion(s32[2048]{0:T(1024)S(1)} %bitcast.201, f32[2048,15]{1,0:T(8,128)S(1)} %copy.377, f32[]{:T(128)} %constant.61.clone.1), kind=kCustom, calls=%fused_computation.68 | custom fusion | flops 30720 | bytes 92164 | tf_op jit(solution)/shard_map/scatter-add | solution.py:38
  44.3 5.8 all-to-all-start.1
  51.2 11.7 %scatter_fusion = f32[15,1024]{0,1:T(8,128)S(1)} fusion(f32[15,1024]{0,1:T(8,128)S(1)} %slice-done.1, s32[2048]{0:T(1024)S(1)} %bitcast.183, f32[2048,15]{1,0:T(8,128)S(1)} %copy.378), kind=kCustom, calls=%fused_computation.19 | custom fusion | flops 30720 | bytes 376832 | tf_op jit(solution)/shard_map/scatter-add | solution.py:38
  67.7 40.7 %all-reduce.4 = (f32[]{:T(128)}, f32[]{:T(128)}) all-reduce(f32[]{:T(128)} %get-tuple-element.95, f32[]{:T(128)} %multiply_reduce_fusion.63), channel_id=1, replica_groups=mesh['rows'=8,'sub'=4] {'rows','sub'}, use_global_device_ids=true, to_apply=%region_10.14 | all-reduce | flops 2 | bytes 16 | tf_op jit(solution)/shard_map/psum | solution.py:115
  154.3 11.8 %scatter_custom_fusion.3 = f32[3,1536]{0,1:T(8,128)S(1)} fusion(s32[2048]{0:T(1024)} %bitcast.202, f32[2048,3]{1,0:T(8,128)S(1)} %copy.389, f32[]{:T(128)} %constant.61.clone.1), kind=kCustom, calls=%fused_computation.64 | custom fusion | flops 6144 | bytes 18944 | tf_op jit(solution)/shard_map/scatter-add | solution.py:38
  167.1 6.4 %all-to-all-start.3 = ((f32[3,32,16]{2,0,1:T(4,128)}), f32[3,32,16]{2,0,1:T(4,128)}, u32[]{:S(2)}, u32[]{:S(2)}) async-start(f32[3,32,16]{2,0,1:T(4,128)} %copy.391), calls=%async_computation.3 | async-start | bytes 131072 | tf_op jit(solution)/shard_map/all_to_all | solution.py:143
  185.8 11.8 %scatter_custom_fusion.6 = f32[15,1536]{0,1:T(8,128)S(1)} fusion(s32[2048]{0:T(1024)} %bitcast.203, f32[2048,15]{1,0:T(8,128)S(1)} %copy.403, f32[]{:T(128)} %constant.61.clone.1), kind=kCustom, calls=%fused_computation.66 | custom fusion | flops 30720 | bytes 92672 | tf_op jit(solution)/shard_map/scatter-add | solution.py:38
  198.5 5.9 all-to-all-start.5
  206.2 11.7 %scatter_fusion.1 = f32[3,1024]{0,1:T(8,128)S(1)} fusion(f32[3,1024]{0,1:T(8,128)S(1)} %slice-done.3, s32[2048]{0:T(1024)S(1)} %bitcast.184, f32[2048,3]{1,0:T(8,128)S(1)} %copy.390), kind=kCustom, calls=%fused_computation.22 | custom fusion | flops 6144 | bytes 81920 | tf_op jit(solution)/shard_map/scatter-add | solution.py:38
  223.0 11.8 %scatter_fusion.2 = f32[15,1024]{0,1:T(8,128)S(1)} fusion(f32[15,1024]{0,1:T(8,128)S(1)} %slice-done, s32[2048]{0:T(1024)S(1)} %bitcast.185, f32[2048,15]{1,0:T(8,128)S(1)} %copy.404), kind=kCustom, calls=%fused_computation.25 | custom fusion | flops 30720 | bytes 376832 | tf_op jit(solution)/shard_map/scatter-add | solution.py:38
  240.8 40.7 %all-reduce.3 = (f32[]{:T(128)}, f32[1]{0:T(128)}) all-reduce(f32[]{:T(128)} %get-tuple-element.72, f32[1]{0:T(128)} %bitcast.41), channel_id=1, replica_groups=mesh['rows'=8,'sub'=4] {'rows','sub'}, use_global_device_ids=true, to_apply=%region_49.56 | all-reduce | flops 2 | bytes 16 | tf_op jit(solution)/shard_map/psum | solution.py:151
  297.7 6.7 %all-to-all-done.6 = f32[3,32,16]{2,0,1:T(4,128)S(1)} async-done(((f32[3,32,16]{2,0,1:T(4,128)}), f32[3,32,16]{2,0,1:T(4,128)S(1)}, u32[]{:S(2)}, u32[]{:S(2)}) %all-to-all-start.6) | async-done | bytes 6176 | tf_op jit(solution)/shard_map/all_to_all | solution.py:139
  312.5 11.8 %scatter_custom_fusion.9 = f32[3,1536]{0,1:T(8,128)S(1)} fusion(s32[2048]{0:T(1024)} %bitcast.204, f32[2048,3]{1,0:T(8,128)S(1)} %copy.414, f32[]{:T(128)} %constant.61.clone.1), kind=kCustom, calls=%fused_computation.62 | custom fusion | flops 6144 | bytes 18944 | tf_op jit(solution)/shard_map/scatter-add | solution.py:38
  328.9 11.9 %scatter_fusion.3 = f32[3,1024]{0,1:T(8,128)S(1)} fusion(f32[3,1024]{0,1:T(8,128)S(1)} %slice-done.4, s32[2048]{0:T(1024)S(1)} %bitcast.186, f32[2048,3]{1,0:T(8,128)S(1)} %copy.415), kind=kCustom, calls=%fused_computation.28 | custom fusion | flops 6144 | bytes 81920 | tf_op jit(solution)/shard_map/scatter-add | solution.py:38
  346.0 40.7 %all-reduce.2 = (f32[]{:T(128)}, f32[2]{0:T(128)S(1)}) all-reduce(f32[]{:T(128)} %get-tuple-element.69, f32[2]{0:T(128)S(1)} %pad_maximum_fusion.3), channel_id=1, replica_groups=mesh['rows'=8,'sub'=4] {'rows','sub'}, use_global_device_ids=true, to_apply=%region_62.69 | all-reduce | flops 3 | bytes 24 | tf_op jit(solution)/shard_map/psum | solution.py:151
  403.9 6.7 %all-to-all-done.8 = f32[3,32,16]{2,0,1:T(4,128)S(1)} async-done(((f32[3,32,16]{2,0,1:T(4,128)}), f32[3,32,16]{2,0,1:T(4,128)S(1)}, u32[]{:S(2)}, u32[]{:S(2)}) %all-to-all-start.8) | async-done | bytes 6176 | tf_op jit(solution)/shard_map/all_to_all | solution.py:139
  417.9 11.8 %scatter_custom_fusion.12 = f32[3,1536]{0,1:T(8,128)S(1)} fusion(s32[2048]{0:T(1024)} %bitcast.205, f32[2048,3]{1,0:T(8,128)S(1)} %copy.428, f32[]{:T(128)} %constant.61.clone.1), kind=kCustom, calls=%fused_computation.60 | custom fusion | flops 6144 | bytes 18944 | tf_op jit(solution)/shard_map/scatter-add | solution.py:38
  434.2 11.7 %scatter_fusion.4 = f32[3,1024]{0,1:T(8,128)S(1)} fusion(f32[3,1024]{0,1:T(8,128)S(1)} %slice-done.5, s32[2048]{0:T(1024)S(1)} %bitcast.187, f32[2048,3]{1,0:T(8,128)S(1)} %copy.429), kind=kCustom, calls=%fused_computation.31 | custom fusion | flops 6144 | bytes 81920 | tf_op jit(solution)/shard_map/scatter-add | solution.py:38
  452.0 40.7 %all-reduce.1 = (f32[]{:T(128)}, f32[3]{0:T(128)S(1)}) all-reduce(f32[]{:T(128)} %get-tuple-element.65, f32[3]{0:T(128)S(1)} %pad_maximum_fusion.4), channel_id=1, replica_groups=mesh['rows'=8,'sub'=4] {'rows','sub'}, use_global_device_ids=true, to_apply=%region_77.84 | all-reduce | flops 4 | bytes 32 | tf_op jit(solution)/shard_map/psum | solution.py:151
  510.2 6.7 %all-to-all-done.10 = f32[3,32,16]{2,0,1:T(4,128)S(1)} async-done(((f32[3,32,16]{2,0,1:T(4,128)}), f32[3,32,16]{2,0,1:T(4,128)S(1)}, u32[]{:S(2)}, u32[]{:S(2)}) %all-to-all-start.10) | async-done | bytes 6176 | tf_op jit(solution)/shard_map/all_to_all | solution.py:139
  524.2 11.8 %scatter_custom_fusion.15 = f32[3,1536]{0,1:T(8,128)S(1)} fusion(s32[2048]{0:T(1024)} %bitcast.206, f32[2048,3]{1,0:T(8,128)S(1)} %copy.442, f32[]{:T(128)} %constant.61.clone.1), kind=kCustom, calls=%fused_computation.58 | custom fusion | flops 6144 | bytes 18944 | tf_op jit(solution)/shard_map/scatter-add | solution.py:38
  540.6 11.7 %scatter_fusion.5 = f32[3,1024]{0,1:T(8,128)S(1)} fusion(f32[3,1024]{0,1:T(8,128)S(1)} %slice-done.2, s32[2048]{0:T(1024)S(1)} %bitcast.188, f32[2048,3]{1,0:T(8,128)S(1)} %copy.443), kind=kCustom, calls=%fused_computation.34 | custom fusion | flops 6144 | bytes 81920 | tf_op jit(solution)/shard_map/scatter-add | solution.py:38
  558.6 40.7 %all-reduce = (f32[]{:T(128)}, f32[4]{0:T(128)S(1)}) all-reduce(f32[]{:T(128)} %get-tuple-element.60, f32[4]{0:T(128)S(1)} %pad_maximum_fusion.5), channel_id=1, replica_groups=mesh['rows'=8,'sub'=4] {'rows','sub'}, use_global_device_ids=true, to_apply=%region_93.100 | all-reduce | flops 5 | bytes 40 | tf_op jit(solution)/shard_map/psum | solution.py:151
  (394 shorter events, 206.1 us)
Async XLA Ops:
  2.5 118.3 %copy-start.45 = (s32[1024]{0:T(1024)}, s32[1024]{0:T(1024)S(1)}, u32[]{:S(2)}) copy-start(s32[1024]{0:T(1024)S(1)} %pad_clamp_fusion) | copy-start | bytes 12292
  3.7 9.9 %copy-start.34 = (f32[36,2048]{1,0:T(8,128)S(1)}, f32[36,2048]{1,0:T(8,128)}, u32[]{:S(2)}) copy-start(f32[36,2048]{1,0:T(8,128)} %param.21) | copy-start | bytes 884740
  4.7 17.5 %all-to-all-start = ((f32[32,1,240]{2,1,0:T(1,128)}), f32[32,1,240]{2,1,0:T(1,128)S(1)}, u32[]{:S(2)}, u32[]{:S(2)}) async-start(f32[32,1,240]{2,1,0:T(1,128)} %reshape.1031), calls=%async_computation | async-start | bytes 65536 | tf_op jit(solution)/shard_map/all_to_all | solution.py:103
  12.8 101.0 %copy-start.30 = (s32[2048]{0:T(1024)}, s32[2048]{0:T(1024)S(1)}, u32[]{:S(2)}) copy-start(s32[2048]{0:T(1024)S(1)} %fusion.27) | copy-start | bytes 24580
  13.5 18.3 %copy-start.54 = (s32[2048,1]{0,1:T(1,128)}, s32[2048,1]{0,1:T(1,128)S(1)}, u32[]{:S(2)}) copy-start(s32[2048,1]{0,1:T(1,128)S(1)} %compare_select_fusion.1) | copy-start | bytes 24580
  13.5 10.7 %copy-start.22 = (s32[2048]{0:T(1024)}, s32[2048]{0:T(1024)S(1)}, u32[]{:S(2)}) copy-start(s32[2048]{0:T(1024)S(1)} %fusion.28) | copy-start | bytes 24580
  13.6 16.1 %copy-start.37 = (pred[2048]{0:T(1024)(128)(4,1)}, pred[2048]{0:T(1024)(128)(4,1)S(1)}, u32[]{:S(2)}) copy-start(pred[2048]{0:T(1024)(128)(4,1)S(1)} %compare_and_fusion) | copy-start | bytes 6148
  13.6 37.0 %copy-start.20 = (s32[2048,1]{0,1:T(1,128)}, s32[2048,1]{0,1:T(1,128)S(1)}, u32[]{:S(2)}) copy-start(s32[2048,1]{0,1:T(1,128)S(1)} %compare_select_fusion) | copy-start | bytes 24580
  13.6 50.4 %copy-start.55 = (s32[512,1]{0,1:T(1,128)}, s32[512,1]{0,1:T(1,128)S(1)}, u32[]{:S(2)}) copy-start(s32[512,1]{0,1:T(1,128)S(1)} %compare_select_fusion.4) | copy-start | bytes 6148
  14.0 16.4 %copy-start.7 = (f32[3,3,2048]{2,1,0:T(4,128)}, f32[3,3,2048]{2,1,0:T(4,128)S(1)}, u32[]{:S(2)}) copy-start(f32[3,3,2048]{2,1,0:T(4,128)S(1)} %get-tuple-element.97) | copy-start | bytes 221188
  14.0 16.4 %copy-start.9 = (f32[3,3,2048]{2,1,0:T(4,128)}, f32[3,3,2048]{2,1,0:T(4,128)S(1)}, u32[]{:S(2)}) copy-start(f32[3,3,2048]{2,1,0:T(4,128)S(1)} %get-tuple-element.98) | copy-start | bytes 221188
  44.3 18.8 %all-to-all-start.1 = ((f32[32,1,240]{2,1,0:T(1,128)}), f32[32,1,240]{2,1,0:T(1,128)S(1)}, u32[]{:S(2)}, u32[]{:S(2)}) async-start(f32[32,1,240]{2,1,0:T(1,128)} %reshape.1033), calls=%async_computation.1 | async-start | bytes 65536 | tf_op jit(solution)/shard_map/all_to_all | solution.py:107
  130.0 12.3 %all-to-all-start.2 = ((f32[3,32,16]{2,0,1:T(4,128)}), f32[3,32,16]{2,0,1:T(4,128)}, u32[]{:S(2)}, u32[]{:S(2)}) async-start(f32[3,32,16]{2,0,1:T(4,128)} %copy.385), calls=%async_computation.2 | async-start | bytes 131072 | tf_op jit(solution)/shard_map/all_to_all | solution.py:139
  142.2 24.8 %all-to-all-start.4 = ((f32[32,1,240]{2,1,0:T(1,128)}), f32[32,1,240]{2,1,0:T(1,128)S(1)}, u32[]{:S(2)}, u32[]{:S(2)}) async-start(f32[32,1,240]{2,1,0:T(1,128)} %reshape.1035), calls=%async_computation.4 | async-start | bytes 65536 | tf_op jit(solution)/shard_map/all_to_all | solution.py:120
  166.1 38.3 %copy-start.3 = (f32[3,1536]{0,1:T(8,128)}, f32[3,1536]{0,1:T(8,128)S(1)}, u32[]{:S(2)}) copy-start(f32[3,1536]{0,1:T(8,128)S(1)} %scatter_custom_fusion.3) | copy-start | bytes 55300
  167.1 31.4 %all-to-all-start.3 = ((f32[3,32,16]{2,0,1:T(4,128)}), f32[3,32,16]{2,0,1:T(4,128)}, u32[]{:S(2)}, u32[]{:S(2)}) async-start(f32[3,32,16]{2,0,1:T(4,128)} %copy.391), calls=%async_computation.3 | async-start | bytes 131072 | tf_op jit(solution)/shard_map/all_to_all | solution.py:143
  197.5 24.4 %copy-start = (f32[15,1536]{0,1:T(8,128)}, f32[15,1536]{0,1:T(8,128)S(1)}, u32[]{:S(2)}) copy-start(f32[15,1536]{0,1:T(8,128)S(1)} %scatter_custom_fusion.6) | copy-start | bytes 276484
  198.5 36.4 %all-to-all-start.5 = ((f32[32,1,240]{2,1,0:T(1,128)}), f32[32,1,240]{2,1,0:T(1,128)S(1)}, u32[]{:S(2)}, u32[]{:S(2)}) async-start(f32[32,1,240]{2,1,0:T(1,128)} %reshape.1037), calls=%async_computation.5 | async-start | bytes 65536 | tf_op jit(solution)/shard_map/all_to_all | solution.py:124
  292.4 12.1 %all-to-all-start.6 = ((f32[3,32,16]{2,0,1:T(4,128)}), f32[3,32,16]{2,0,1:T(4,128)S(1)}, u32[]{:S(2)}, u32[]{:S(2)}) async-start(f32[3,32,16]{2,0,1:T(4,128)} %copy.410), calls=%async_computation.6 | async-start | bytes 131072 | tf_op jit(solution)/shard_map/all_to_all | solution.py:139
  325.2 15.8 %all-to-all-start.7 = ((f32[3,32,16]{2,0,1:T(4,128)}), f32[3,32,16]{2,0,1:T(4,128)S(1)}, u32[]{:S(2)}, u32[]{:S(2)}) async-start(f32[3,32,16]{2,0,1:T(4,128)} %copy.416), calls=%async_computation.7 | async-start | bytes 131072 | tf_op jit(solution)/shard_map/all_to_all | solution.py:143
  398.5 12.1 %all-to-all-start.8 = ((f32[3,32,16]{2,0,1:T(4,128)}), f32[3,32,16]{2,0,1:T(4,128)S(1)}, u32[]{:S(2)}, u32[]{:S(2)}) async-start(f32[3,32,16]{2,0,1:T(4,128)} %copy.424), calls=%async_computation.8 | async-start | bytes 131072 | tf_op jit(solution)/shard_map/all_to_all | solution.py:139
  430.6 15.5 %all-to-all-start.9 = ((f32[3,32,16]{2,0,1:T(4,128)}), f32[3,32,16]{2,0,1:T(4,128)S(1)}, u32[]{:S(2)}, u32[]{:S(2)}) async-start(f32[3,32,16]{2,0,1:T(4,128)} %copy.430), calls=%async_computation.9 | async-start | bytes 131072 | tf_op jit(solution)/shard_map/all_to_all | solution.py:143
  504.9 12.0 %all-to-all-start.10 = ((f32[3,32,16]{2,0,1:T(4,128)}), f32[3,32,16]{2,0,1:T(4,128)S(1)}, u32[]{:S(2)}, u32[]{:S(2)}) async-start(f32[3,32,16]{2,0,1:T(4,128)} %copy.438), calls=%async_computation.10 | async-start | bytes 131072 | tf_op jit(solution)/shard_map/all_to_all | solution.py:139
  536.9 15.5 %all-to-all-start.11 = ((f32[3,32,16]{2,0,1:T(4,128)}), f32[3,32,16]{2,0,1:T(4,128)S(1)}, u32[]{:S(2)}, u32[]{:S(2)}) async-start(f32[3,32,16]{2,0,1:T(4,128)} %copy.444), calls=%async_computation.11 | async-start | bytes 131072 | tf_op jit(solution)/shard_map/all_to_all | solution.py:143
  (50 other events, 115.0 us)
where the time goes:
time: 619 us; the launch traced here: 608 us
  blocking collectives  204 us (33%)
  other arithmetic  195 us (32%)
  local copies, waits for them, and re-layouts  120 us (19%)
  starting transfers between devices  54.6 us (9%)
  waiting for transfers between devices  24 us (4%)
  between operations  11.7 us (2%)
    psum x4, blocking collectives, on_device(): lax.psum((local_dots, jnp.sum(image_vec * image_vec)), ('rows', 'sub'))  163 us
    scatter-add x18, other arithmetic, add_columns(): return total.at[:, index].add(values, mode='drop')  156 us
    gather x18, local copies, waits for them, and re-layouts, take_columns(): return jnp.take(table, index, axis=1, mode='fill', fill_value=0.0)  73 us
    psum x1, blocking collectives, on_device(): total_square = lax.psum(jnp.sum(gradient * gradient), ('rows', 'sub'))  40.7 us
    all_to_all x4, waiting for transfers between devices, on_device(): lax.all_to_all(pack_rows(vector, send_row), ('rows', 'sub'), split_axis=1...  23.9 us
    all_to_all x4, starting transfers between devices, on_device(): lax.all_to_all(pack_rows(vector, send_row), ('rows', 'sub'), split_axis=1...  18.9 us
    unnamed x121, local copies, waits for them, and re-layouts  14.4 us
    all_to_all x4, starting transfers between devices, on_device(): lax.all_to_all(far_vector.reshape(DIM, -1), ('rows', 'sub'), split_axis=1...  14.1 us
  transfers between devices with their start and end apart: 12, of which 4 were waited for; matrix products, arithmetic and copies ran while one was open for 22% of the time, Pallas kernels for 0%

commit v1 on v0

--- a/solution.py
+++ b/solution.py
@@ -136,9 +136,10 @@
     beta_list = []
     for iteration in range(LANCZOS):
         vector = krylov_basis[-1]
-        halo_vector = lax.all_to_all(
-            pack_rows(vector, send_row), ("rows", "sub"), split_axis=1, concat_axis=1, tiled=True
-        )
+        block = pack_rows(vector, send_row)
+        pieces = jnp.split(block, lax.axis_size(("rows", "sub")), axis=1)
+        got = lax.all_to_all(jnp.stack(pieces), ("rows", "sub"), 0, 0)
+        halo_vector = jnp.concatenate(got, axis=1)
         near_vector, far_vector = split_product(vector, halo_vector)
         returned_vector = lax.all_to_all(
             far_vector.reshape(DIM, -1), ("rows", "sub"), split_axis=1, concat_axis=1, tiled=True

time: 619 us -> 713 us (1.15)
  local copies, waits for them, and re-layouts: 120 us -> 212 us
    unnamed x121 -> x303, local copies, waits for them, and re-layouts: 14.4 us -> 96.6 us
    split x0 -> x136, local copies, waits for them, and re-layouts: none -> 12.3 us  [on_device(): pieces = jnp.split(block, lax.axis_size(('rows', 'sub')), axis=1)]
  transfers between devices with their start and end apart: 12 -> 12, of which waited for: 4 -> 4; matrix products, arithmetic and copies ran while one was open for 22% -> 19% of each run, Pallas kernels for 0% -> 0%
where the time goes in v1:
time: 713 us; the launch traced here: 701 us
  local copies, waits for them, and re-layouts  212 us (30%)
  blocking collectives  203 us (28%)
  other arithmetic  195 us (27%)
  starting transfers between devices  54.6 us (8%)
  waiting for transfers between devices  23.9 us (3%)
  between operations  11.9 us (2%)
    psum x4, blocking collectives, on_device(): lax.psum((local_dots, jnp.sum(image_vec * image_vec)), ('rows', 'sub'))  163 us
    scatter-add x18, other arithmetic, add_columns(): return total.at[:, index].add(values, mode='drop')  157 us
    unnamed x303, local copies, waits for them, and re-layouts  96.6 us
    gather x18, local copies, waits for them, and re-layouts, take_columns(): return jnp.take(table, index, axis=1, mode='fill', fill_value=0.0)  72.4 us
    psum x1, blocking collectives, on_device(): total_square = lax.psum(jnp.sum(gradient * gradient), ('rows', 'sub'))  40.7 us
    all_to_all x4, waiting for transfers between devices, on_device(): got = lax.all_to_all(jnp.stack(pieces), ('rows', 'sub'), 0, 0)  23.9 us
    all_to_all x4, starting transfers between devices, on_device(): got = lax.all_to_all(jnp.stack(pieces), ('rows', 'sub'), 0, 0)  18.9 us
  transfers between devices with their start and end apart: 12, of which 4 were waited for; matrix products, arithmetic and copies ran while one was open for 19% of the time, Pallas kernels for 0%

profile of v1, /device:TPU:0, one launch (start us, length us, event | category | flops | bytes accessed | tf_op | source)
XLA Modules:
  0.0 701.1 jit_solution(383724269607353366)
XLA Ops:
  4.7 7.3 %all-to-all-start = ((f32[32,1,240]{2,1,0:T(1,128)}), f32[32,1,240]{2,1,0:T(1,128)S(1)}, u32[]{:S(2)}, u32[]{:S(2)}) async-start(f32[32,1,240]{2,1,0:T(1,128)} %reshape.1019), calls=%async_computation | async-start | bytes 65536 | tf_op jit(solution)/shard_map/all_to_all | solution.py:103
  31.8 11.7 %scatter_custom_fusion = f32[15,1536]{0,1:T(8,128)S(1)} fusion(s32[2048]{0:T(1024)S(1)} %bitcast.456, f32[2048,15]{1,0:T(8,128)S(1)} %copy.1525, f32[]{:T(128)} %constant.61.clone.1), kind=kCustom, calls=%fused_computation.68 | custom fusion | flops 30720 | bytes 92164 | tf_op jit(solution)/shard_map/scatter-add | solution.py:38
  44.3 5.8 all-to-all-start.1
  51.2 11.7 %scatter_fusion = f32[15,1024]{0,1:T(8,128)S(1)} fusion(f32[15,1024]{0,1:T(8,128)S(1)} %slice-done.1, s32[2048]{0:T(1024)S(1)} %bitcast.435, f32[2048,15]{1,0:T(8,128)S(1)} %copy.1526), kind=kCustom, calls=%fused_computation.19 | custom fusion | flops 30720 | bytes 376832 | tf_op jit(solution)/shard_map/scatter-add | solution.py:38
  67.7 40.7 %all-reduce.4 = (f32[]{:T(128)}, f32[]{:T(128)}) all-reduce(f32[]{:T(128)} %get-tuple-element.95, f32[]{:T(128)} %multiply_reduce_fusion.63), channel_id=1, replica_groups=mesh['rows'=8,'sub'=4] {'rows','sub'}, use_global_device_ids=true, to_apply=%region_10.14 | all-reduce | flops 2 | bytes 16 | tf_op jit(solution)/shard_map/psum | solution.py:115
  185.3 11.8 %scatter_custom_fusion.3 = f32[3,1536]{0,1:T(8,128)S(1)} fusion(s32[2048]{0:T(1024)} %bitcast.457, f32[2048,3]{1,0:T(8,128)S(1)} %copy.1568, f32[]{:T(128)} %constant.61.clone.1), kind=kCustom, calls=%fused_computation.64 | custom fusion | flops 6144 | bytes 18944 | tf_op jit(solution)/shard_map/scatter-add | solution.py:38
  198.1 6.4 all-to-all-start.3
  216.8 11.8 %scatter_custom_fusion.6 = f32[15,1536]{0,1:T(8,128)S(1)} fusion(s32[2048]{0:T(1024)} %bitcast.458, f32[2048,15]{1,0:T(8,128)S(1)} %copy.1582, f32[]{:T(128)} %constant.61.clone.1), kind=kCustom, calls=%fused_computation.66 | custom fusion | flops 30720 | bytes 92672 | tf_op jit(solution)/shard_map/scatter-add | solution.py:38
  229.5 5.9 all-to-all-start.5
  237.2 11.7 %scatter_fusion.1 = f32[3,1024]{0,1:T(8,128)S(1)} fusion(f32[3,1024]{0,1:T(8,128)S(1)} %slice-done.3, s32[2048]{0:T(1024)S(1)} %bitcast.436, f32[2048,3]{1,0:T(8,128)S(1)} %copy.1569), kind=kCustom, calls=%fused_computation.22 | custom fusion | flops 6144 | bytes 81920 | tf_op jit(solution)/shard_map/scatter-add | solution.py:38
  254.0 11.8 %scatter_fusion.2 = f32[15,1024]{0,1:T(8,128)S(1)} fusion(f32[15,1024]{0,1:T(8,128)S(1)} %slice-done, s32[2048]{0:T(1024)S(1)} %bitcast.437, f32[2048,15]{1,0:T(8,128)S(1)} %copy.1583), kind=kCustom, calls=%fused_computation.25 | custom fusion | flops 30720 | bytes 376832 | tf_op jit(solution)/shard_map/scatter-add | solution.py:38
  271.8 40.7 %all-reduce.3 = (f32[]{:T(128)}, f32[1]{0:T(128)}) all-reduce(f32[]{:T(128)} %get-tuple-element.72, f32[1]{0:T(128)} %bitcast.73), channel_id=1, replica_groups=mesh['rows'=8,'sub'=4] {'rows','sub'}, use_global_device_ids=true, to_apply=%region_49.56 | all-reduce | flops 2 | bytes 16 | tf_op jit(solution)/shard_map/psum | solution.py:152
  349.7 6.7 all-to-all-done.6
  364.5 11.8 %scatter_custom_fusion.9 = f32[3,1536]{0,1:T(8,128)S(1)} fusion(s32[2048]{0:T(1024)} %bitcast.459, f32[2048,3]{1,0:T(8,128)S(1)} %copy.1624, f32[]{:T(128)} %constant.61.clone.1), kind=kCustom, calls=%fused_computation.62 | custom fusion | flops 6144 | bytes 18944 | tf_op jit(solution)/shard_map/scatter-add | solution.py:38
  380.9 11.9 %scatter_fusion.3 = f32[3,1024]{0,1:T(8,128)S(1)} fusion(f32[3,1024]{0,1:T(8,128)S(1)} %slice-done.4, s32[2048]{0:T(1024)S(1)} %bitcast.438, f32[2048,3]{1,0:T(8,128)S(1)} %copy.1625), kind=kCustom, calls=%fused_computation.28 | custom fusion | flops 6144 | bytes 81920 | tf_op jit(solution)/shard_map/scatter-add | solution.py:38
  398.0 40.7 %all-reduce.2 = (f32[]{:T(128)}, f32[2]{0:T(128)S(1)}) all-reduce(f32[]{:T(128)} %get-tuple-element.69, f32[2]{0:T(128)S(1)} %pad_maximum_fusion.3), channel_id=1, replica_groups=mesh['rows'=8,'sub'=4] {'rows','sub'}, use_global_device_ids=true, to_apply=%region_62.69 | all-reduce | flops 3 | bytes 24 | tf_op jit(solution)/shard_map/psum | solution.py:152
  476.3 6.7 all-to-all-done.8
  490.3 11.8 %scatter_custom_fusion.12 = f32[3,1536]{0,1:T(8,128)S(1)} fusion(s32[2048]{0:T(1024)} %bitcast.460, f32[2048,3]{1,0:T(8,128)S(1)} %copy.1669, f32[]{:T(128)} %constant.61.clone.1), kind=kCustom, calls=%fused_computation.60 | custom fusion | flops 6144 | bytes 18944 | tf_op jit(solution)/shard_map/scatter-add | solution.py:38
  506.6 11.9 %scatter_fusion.4 = f32[3,1024]{0,1:T(8,128)S(1)} fusion(f32[3,1024]{0,1:T(8,128)S(1)} %slice-done.5, s32[2048]{0:T(1024)S(1)} %bitcast.439, f32[2048,3]{1,0:T(8,128)S(1)} %copy.1670), kind=kCustom, calls=%fused_computation.31 | custom fusion | flops 6144 | bytes 81920 | tf_op jit(solution)/shard_map/scatter-add | solution.py:38
  524.4 40.7 %all-reduce.1 = (f32[]{:T(128)}, f32[3]{0:T(128)S(1)}) all-reduce(f32[]{:T(128)} %get-tuple-element.65, f32[3]{0:T(128)S(1)} %pad_maximum_fusion.4), channel_id=1, replica_groups=mesh['rows'=8,'sub'=4] {'rows','sub'}, use_global_device_ids=true, to_apply=%region_77.84 | all-reduce | flops 4 | bytes 32 | tf_op jit(solution)/shard_map/psum | solution.py:152
  603.0 6.7 all-to-all-done.10
  617.0 11.8 %scatter_custom_fusion.15 = f32[3,1536]{0,1:T(8,128)S(1)} fusion(s32[2048]{0:T(1024)} %bitcast.461, f32[2048,3]{1,0:T(8,128)S(1)} %copy.1714, f32[]{:T(128)} %constant.61.clone.1), kind=kCustom, calls=%fused_computation.58 | custom fusion | flops 6144 | bytes 18944 | tf_op jit(solution)/shard_map/scatter-add | solution.py:38
  633.3 12.0 %scatter_fusion.5 = f32[3,1024]{0,1:T(8,128)S(1)} fusion(f32[3,1024]{0,1:T(8,128)S(1)} %slice-done.2, s32[2048]{0:T(1024)S(1)} %bitcast.440, f32[2048,3]{1,0:T(8,128)S(1)} %copy.1715), kind=kCustom, calls=%fused_computation.34 | custom fusion | flops 6144 | bytes 81920 | tf_op jit(solution)/shard_map/scatter-add | solution.py:38
  651.7 40.7 %all-reduce = (f32[]{:T(128)}, f32[4]{0:T(128)S(1)}) all-reduce(f32[]{:T(128)} %get-tuple-element.60, f32[4]{0:T(128)S(1)} %pad_maximum_fusion.5), channel_id=1, replica_groups=mesh['rows'=8,'sub'=4] {'rows','sub'}, use_global_device_ids=true, to_apply=%region_93.100 | all-reduce | flops 5 | bytes 40 | tf_op jit(solution)/shard_map/psum | solution.py:152
  (712 shorter events, 298.5 us)
Async XLA Ops:
  1.4 120.4 %copy-start.79 = (pred[512]{0:T(512)(128)(4,1)}, pred[512]{0:T(512)(128)(4,1)S(1)}, u32[]{:S(2)}) copy-start(pred[512]{0:T(512)(128)(4,1)S(1)} %compare_and_fusion.2) | copy-start | bytes 1540
  2.5 118.2 %copy-start.44 = (s32[1024]{0:T(1024)}, s32[1024]{0:T(1024)S(1)}, u32[]{:S(2)}) copy-start(s32[1024]{0:T(1024)S(1)} %pad_clamp_fusion) | copy-start | bytes 12292
  4.7 17.5 %all-to-all-start = ((f32[32,1,240]{2,1,0:T(1,128)}), f32[32,1,240]{2,1,0:T(1,128)S(1)}, u32[]{:S(2)}, u32[]{:S(2)}) async-start(f32[32,1,240]{2,1,0:T(1,128)} %reshape.1019), calls=%async_computation | async-start | bytes 65536 | tf_op jit(solution)/shard_map/all_to_all | solution.py:103
  12.8 101.0 %copy-start.30 = (s32[2048]{0:T(1024)}, s32[2048]{0:T(1024)S(1)}, u32[]{:S(2)}) copy-start(s32[2048]{0:T(1024)S(1)} %fusion.27) | copy-start | bytes 24580
  13.5 18.3 %copy-start.83 = (s32[2048,1]{0,1:T(1,128)}, s32[2048,1]{0,1:T(1,128)S(1)}, u32[]{:S(2)}) copy-start(s32[2048,1]{0,1:T(1,128)S(1)} %compare_select_fusion.1) | copy-start | bytes 24580
  13.5 10.7 %copy-start.22 = (s32[2048]{0:T(1024)}, s32[2048]{0:T(1024)S(1)}, u32[]{:S(2)}) copy-start(s32[2048]{0:T(1024)S(1)} %fusion.28) | copy-start | bytes 24580
  13.6 16.1 %copy-start.36 = (pred[2048]{0:T(1024)(128)(4,1)}, pred[2048]{0:T(1024)(128)(4,1)S(1)}, u32[]{:S(2)}) copy-start(pred[2048]{0:T(1024)(128)(4,1)S(1)} %compare_and_fusion) | copy-start | bytes 6148
  13.6 37.0 %copy-start.20 = (s32[2048,1]{0,1:T(1,128)}, s32[2048,1]{0,1:T(1,128)S(1)}, u32[]{:S(2)}) copy-start(s32[2048,1]{0,1:T(1,128)S(1)} %compare_select_fusion) | copy-start | bytes 24580
  13.6 50.4 %copy-start.84 = (s32[512,1]{0,1:T(1,128)}, s32[512,1]{0,1:T(1,128)S(1)}, u32[]{:S(2)}) copy-start(s32[512,1]{0,1:T(1,128)S(1)} %compare_select_fusion.4) | copy-start | bytes 6148
  14.0 16.4 %copy-start.7 = (f32[3,3,2048]{2,1,0:T(4,128)}, f32[3,3,2048]{2,1,0:T(4,128)S(1)}, u32[]{:S(2)}) copy-start(f32[3,3,2048]{2,1,0:T(4,128)S(1)} %get-tuple-element.97) | copy-start | bytes 221188
  14.0 16.4 %copy-start.9 = (f32[3,3,2048]{2,1,0:T(4,128)}, f32[3,3,2048]{2,1,0:T(4,128)S(1)}, u32[]{:S(2)}) copy-start(f32[3,3,2048]{2,1,0:T(4,128)S(1)} %get-tuple-element.98) | copy-start | bytes 221188
  44.3 18.8 %all-to-all-start.1 = ((f32[32,1,240]{2,1,0:T(1,128)}), f32[32,1,240]{2,1,0:T(1,128)S(1)}, u32[]{:S(2)}, u32[]{:S(2)}) async-start(f32[32,1,240]{2,1,0:T(1,128)} %reshape.1021), calls=%async_computation.1 | async-start | bytes 65536 | tf_op jit(solution)/shard_map/all_to_all | solution.py:107
  161.0 12.3 %all-to-all-start.2 = ((f32[32,3,16]{2,1,0:T(4,128)}), f32[32,3,16]{2,1,0:T(4,128)}, u32[]{:S(2)}, u32[]{:S(2)}) async-start(f32[32,3,16]{2,1,0:T(4,128)} %constant_dynamic-update-slice_fusion), calls=%async_computation.2 | async-start | bytes 131072 | tf_op jit(solution)/shard_map/all_to_all | solution.py:141
  173.3 24.8 %all-to-all-start.4 = ((f32[32,1,240]{2,1,0:T(1,128)}), f32[32,1,240]{2,1,0:T(1,128)S(1)}, u32[]{:S(2)}, u32[]{:S(2)}) async-start(f32[32,1,240]{2,1,0:T(1,128)} %reshape.1023), calls=%async_computation.4 | async-start | bytes 65536 | tf_op jit(solution)/shard_map/all_to_all | solution.py:120
  197.1 38.3 %copy-start.3 = (f32[3,1536]{0,1:T(8,128)}, f32[3,1536]{0,1:T(8,128)S(1)}, u32[]{:S(2)}) copy-start(f32[3,1536]{0,1:T(8,128)S(1)} %scatter_custom_fusion.3) | copy-start | bytes 55300
  198.1 31.4 %all-to-all-start.3 = ((f32[3,32,16]{2,0,1:T(4,128)}), f32[3,32,16]{2,0,1:T(4,128)}, u32[]{:S(2)}, u32[]{:S(2)}) async-start(f32[3,32,16]{2,0,1:T(4,128)} %copy.1570), calls=%async_computation.3 | async-start | bytes 131072 | tf_op jit(solution)/shard_map/all_to_all | solution.py:144
  228.5 24.4 %copy-start = (f32[15,1536]{0,1:T(8,128)}, f32[15,1536]{0,1:T(8,128)S(1)}, u32[]{:S(2)}) copy-start(f32[15,1536]{0,1:T(8,128)S(1)} %scatter_custom_fusion.6) | copy-start | bytes 276484
  229.5 36.4 %all-to-all-start.5 = ((f32[32,1,240]{2,1,0:T(1,128)}), f32[32,1,240]{2,1,0:T(1,128)S(1)}, u32[]{:S(2)}, u32[]{:S(2)}) async-start(f32[32,1,240]{2,1,0:T(1,128)} %reshape.1025), calls=%async_computation.5 | async-start | bytes 65536 | tf_op jit(solution)/shard_map/all_to_all | solution.py:124
  344.4 12.1 %all-to-all-start.6 = ((f32[32,3,16]{2,1,0:T(4,128)}), f32[32,3,16]{2,1,0:T(4,128)S(1)}, u32[]{:S(2)}, u32[]{:S(2)}) async-start(f32[32,3,16]{2,1,0:T(4,128)} %constant_dynamic-update-slice_fusion.32), calls=%async_computation.6 | async-start | bytes 131072 | tf_op jit(solution)/shard_map/all_to_all | solution.py:141
  377.2 15.8 %all-to-all-start.7 = ((f32[3,32,16]{2,0,1:T(4,128)}), f32[3,32,16]{2,0,1:T(4,128)S(1)}, u32[]{:S(2)}, u32[]{:S(2)}) async-start(f32[3,32,16]{2,0,1:T(4,128)} %copy.1626), calls=%async_computation.7 | async-start | bytes 131072 | tf_op jit(solution)/shard_map/all_to_all | solution.py:144
  470.9 12.1 %all-to-all-start.8 = ((f32[32,3,16]{2,1,0:T(4,128)}), f32[32,3,16]{2,1,0:T(4,128)S(1)}, u32[]{:S(2)}, u32[]{:S(2)}) async-start(f32[32,3,16]{2,1,0:T(4,128)} %constant_dynamic-update-slice_fusion.64), calls=%async_computation.8 | async-start | bytes 131072 | tf_op jit(solution)/shard_map/all_to_all | solution.py:141
  503.0 15.8 %all-to-all-start.9 = ((f32[3,32,16]{2,0,1:T(4,128)}), f32[3,32,16]{2,0,1:T(4,128)S(1)}, u32[]{:S(2)}, u32[]{:S(2)}) async-start(f32[3,32,16]{2,0,1:T(4,128)} %copy.1671), calls=%async_computation.9 | async-start | bytes 131072 | tf_op jit(solution)/shard_map/all_to_all | solution.py:144
  597.7 12.0 %all-to-all-start.10 = ((f32[32,3,16]{2,1,0:T(4,128)}), f32[32,3,16]{2,1,0:T(4,128)S(1)}, u32[]{:S(2)}, u32[]{:S(2)}) async-start(f32[32,3,16]{2,1,0:T(4,128)} %constant_dynamic-update-slice_fusion.96), calls=%async_computation.10 | async-start | bytes 131072 | tf_op jit(solution)/shard_map/all_to_all | solution.py:141
  629.7 15.8 %all-to-all-start.11 = ((f32[3,32,16]{2,0,1:T(4,128)}), f32[3,32,16]{2,0,1:T(4,128)S(1)}, u32[]{:S(2)}, u32[]{:S(2)}) async-start(f32[3,32,16]{2,0,1:T(4,128)} %copy.1716), calls=%async_computation.11 | async-start | bytes 131072 | tf_op jit(solution)/shard_map/all_to_all | solution.py:144
  (79 other events, 137.3 us)
